TPU v7x, 32 devices: a whole 2x2x4 slice. The times are simulated.
32 devices in a mesh: dp: 8 (over y, x, core), mp: 4 (over z).
Axes of the slice: x: 2, y: 2, z: 4, core: 2. Of those that a mesh axis runs over, the one named last changes fastest.
Arguments:
- doc_ids: int32 [8, 512], P('dp'), may hold values from 0 to 128255
- doc_lengths: int32 [8], P('dp'), may hold values from 128 to 512
- activations: bfloat16 [4096, 4096], P('dp'), may hold values from -6 to 6
- out_grads: bfloat16 [4096, 14336], P('dp'), may hold values from -0.29882812 to 0.29882812
- input_basis: bfloat16 [4096, 2048], P(None, 'mp'), may hold values from -0.09375 to 0.09375
- output_basis: bfloat16 [14336, 7168], P('dp', 'mp'), may hold values from -0.046875 to 0.046875
- eigenvalues: bfloat16 [2048, 7168], P(None, 'mp'), may hold values from 0.5 to 50
- query_left: bfloat16 [32, 32, 2048], P('dp'), may hold values from -0.125 to 0.125
- query_right: bfloat16 [32, 32, 7168], P('dp', None, 'mp'), may hold values from -0.0625 to 0.0625
Outputs:
- scores: float32 [8, 32], P('dp')
Inputs may be any that keep to these rules, and one draw needn't show every extreme that they name: `doc_lengths`: the live tokens are the first ones of each document.
All inputs are finite; a program needn't handle non-finite values.
Results may differ from a plain program's by a relative error of at most 0.023.
Values may be sent and summed in bfloat16 or wider, within the bound.
A program may use at most 192 MiB of HBM per device.

v0:
```python
import jax
import jax.numpy as jnp
from jax import lax
from jax.sharding import PartitionSpec as P

damping = 0.5


def token_weights(doc_ids, doc_lengths):
    positions = jnp.arange(doc_ids.shape[1], dtype=jnp.int32)
    active = positions[None, :] < doc_lengths[:, None]
    matches = (doc_ids[:, :, None] == doc_ids[:, None, :]) & active[:, None, :]
    repeats = jnp.sum(matches.astype(jnp.float32), axis=2)
    return jnp.where(active, 1.0 / jnp.maximum(repeats, 1.0), 0.0)


def per_device(
    doc_ids,
    doc_lengths,
    activations,
    out_grads,
    input_basis,
    output_basis,
    eigenvalues,
    query_left,
    query_right,
):
    out_cols = output_basis.shape[1]
    rotated_share = jnp.dot(activations, input_basis, preferred_element_type=jnp.float32).astype(
        jnp.bfloat16
    )
    rotated_in = lax.all_gather(rotated_share, "mp", axis=1, tiled=True)
    columns = lax.all_to_all(out_grads, "dp", split_axis=1, concat_axis=0, tiled=True)
    summed = lax.psum_scatter(
        jnp.dot(columns, output_basis, preferred_element_type=jnp.float32).astype(jnp.bfloat16),
        "dp",
        scatter_dimension=0,
        tiled=True,
    )
    weights = token_weights(doc_ids, doc_lengths)
    docs_here = doc_ids.shape[0]
    acts_doc = rotated_in.reshape(docs_here, -1, rotated_in.shape[1])
    grads_doc = summed.reshape(docs_here, -1, out_cols)
    scaled = (weights[:, :, None] * grads_doc.astype(jnp.float32)).astype(jnp.bfloat16)
    gradient = jnp.einsum("dti,dtj->dij", acts_doc, scaled, preferred_element_type=jnp.float32)
    conditioned = (gradient / (eigenvalues.astype(jnp.float32) + damping)).astype(jnp.bfloat16)
    rank_rows = query_left.shape[1]
    left_part = lax.all_gather(query_left, "dp", axis=0, tiled=True)
    right_part = lax.all_gather(query_right, "dp", axis=0, tiled=True)
    number = left_part.shape[0]
    left_rows = left_part.reshape(number * rank_rows, left_part.shape[2])
    right_rows = right_part.reshape(number * rank_rows, right_part.shape[2]).astype(jnp.float32)
    mixture = jnp.einsum("ri,dij->drj", left_rows, conditioned, preferred_element_type=jnp.float32)
    values = jnp.sum((mixture * right_rows[None]).reshape(docs_here, number, -1), axis=2)
    return lax.psum(values, "mp")


def solution(mesh):
    return jax.shard_map(
        per_device,
        mesh=mesh,
        in_specs=(
            P("dp", None),
            P("dp"),
            P("dp", None),
            P("dp", None),
            P(None, "mp"),
            P("dp", "mp"),
            P(None, "mp"),
            P("dp", None, None),
            P("dp", None, "mp"),
        ),
        out_specs=P("dp", None),
        check_vma=False,
    )
```

profile of v0, /device:TPU:0, one launch (start us, length us, event | category | flops | bytes accessed | tf_op | source)
XLA Modules:
  0.0 409.6 jit_solution(17460435752555275028)
XLA Ops:
  6.5 20.0 %copy.18 = bf16[512,14336]{0,1:T(8,128)(2,1)} copy(bf16[512,14336]{1,0:T(8,128)(2,1)} %param.12) | data formatting | bytes 29360128 | tf_op args[3]
  26.5 5.6 %all-to-all-start = ((bf16[512,8,1792]{0,2,1:T(8,128)(2,1)}), bf16[512,8,1792]{0,2,1:T(8,128)(2,1)}, u32[]{:S(2)}, u32[]{:S(2)}) async-start(bf16[512,8,1792]{0,2,1:T(8,128)(2,1)} %bitcast.25), calls=%async_computation | async-start | bytes 29360128 | tf_op jit(solution)/shard_map/all_to_all | solution.py:33
  32.1 0.0 all-gather.8.cloned.1.call-start
  32.1 0.7 all-gather.8.cloned.1.call-update
  32.8 0.0 all-gather.4.cloned.1.call-start
  32.8 6.6 %convolution_convert_fusion.1 = bf16[512,512]{1,0:T(8,128)(2,1)} fusion(bf16[512,4096]{1,0:T(8,128)(2,1)} %param.11, bf16[4096,512]{1,0:T(8,128)(2,1)} %param.13), kind=kOutput, calls=%fused_computation.9 | convolution fusion | flops 2147745792 | bytes 8912896 | tf_op jit(solution)/shard_map/dot_general | solution.py:29
  39.4 0.0 all-gather.4.cloned.1.call-update
  39.5 0.0 all-gather.6.cloned.1.call-start
  39.5 0.7 all-gather.6.cloned.1.call-update
  40.2 0.0 reduce-scatter.2.cloned.1.call-start
  40.3 174.3 %all-to-all-done = bf16[512,8,1792]{0,2,1:T(8,128)(2,1)} async-done(((bf16[512,8,1792]{0,2,1:T(8,128)(2,1)}), bf16[512,8,1792]{0,2,1:T(8,128)(2,1)}, u32[]{:S(2)}, u32[]{:S(2)}) %all-to-all-start) | async-done | bytes 14680096 | tf_op jit(solution)/shard_map/all_to_all | solution.py:33
  214.6 18.9 %copy.19 = bf16[8,512,1792]{2,1,0:T(8,128)(2,1)} copy(bf16[8,512,1792]{1,2,0:T(8,128)(2,1)} %bitcast.3) | data formatting | bytes 29360128 | tf_op jit(solution)/shard_map/all_to_all | solution.py:33
  233.4 33.0 %convolution_convert_fusion = bf16[4096,1792]{1,0:T(8,128)(2,1)} fusion(bf16[4096,1792]{1,0:T(8,128)(2,1)} %bitcast.26, bf16[1792,1792]{1,0:T(8,128)(2,1)} %param.14), kind=kOutput, calls=%fused_computation | convolution fusion | flops 26314014720 | bytes 35782656 | tf_op jit(solution)/shard_map/dot_general | solution.py:35
  266.5 0.0 reduce-scatter.2.cloned.1.call-update
  267.1 0.0 copy-done
  267.2 0.3 convert_reduce_fusion
  267.5 0.0 all-gather.8.cloned.1.call-done
  267.5 6.2 %bitcast_convert_fusion = f32[1,1024,1792]{2,1,0:T(8,128)} fusion(bf16[1,1024,1792]{2,1,0:T(8,128)(2,1)} %bitcast.27), kind=kLoop, calls=%fused_computation.6 | loop fusion | flops 1835008 | bytes 11010048 | tf_op jit(solution)/shard_map/convert_element_type | solution.py:52
  273.7 9.0 %copy.20 = f32[1,1024,1792]{1,2,0:T(8,128)} copy(f32[1,1024,1792]{2,1,0:T(8,128)} %bitcast_convert_fusion) | data formatting | bytes 14680064 | tf_op jit(solution)/shard_map/convert_element_type | solution.py:52
  282.7 88.7 %reduce-scatter.2.cloned.1.call-done = bf16[512,1792]{1,0:T(8,128)(2,1)} async-done(((bf16[4096,1792]{1,0:T(8,128)(2,1)}), bf16[512,1792]{1,0:T(8,128)(2,1)}) %reduce-scatter.2.cloned.1.call-update) | async-done | bytes 1835024 | tf_op jit(solution)/shard_map/reduce_scatter | solution.py:34
  371.5 19.2 %fusion = f32[1024]{0:T(1024)S(1)} fusion(f32[1,1024,1792]{1,2,0:T(8,128)} %copy.20, bf16[1024,2048]{1,0:T(8,128)(2,1)} %bitcast.30, bf16[2048,1792]{1,0:T(8,128)(2,1)} %param.15, bf16[512,2048]{1,0:T(8,128)(2,1)} %all-gather.4.cloned.1.call-done, bf16[512,1792]{1,0:T(8,128)(2,1)} %reduce-scatter.2.cloned.1.call-done, f32[512]{0:T(512)S(1)} %divide_select_fusion), kind=kOutput, calls=%fused_computation.3 | convolution fusion | flops 11295390720 | bytes 22812672 | tf_op jit(solution)/shard_map/ri,dij->drj/dot_general | solution.py:53
  390.7 0.1 reduce_sum.29
  390.7 0.1 reduce_sum.30
  390.9 12.2 %psum.7 = f32[1,32]{1,0:T(1,128)} all-reduce(f32[1,32]{1,0:T(1,128)S(1)} %bitcast.29), channel_id=1, replica_groups=mesh['dp'=8,'mp'=4] {'mp'}, use_global_device_ids=true, to_apply=%region_4.5 | all-reduce | flops 32 | bytes 256 | tf_op jit(solution)/shard_map/psum | solution.py:55
  (5 shorter events, 0.0 us)
Async XLA Ops:
  26.5 188.1 %all-to-all-start = ((bf16[512,8,1792]{0,2,1:T(8,128)(2,1)}), bf16[512,8,1792]{0,2,1:T(8,128)(2,1)}, u32[]{:S(2)}, u32[]{:S(2)}) async-start(bf16[512,8,1792]{0,2,1:T(8,128)(2,1)} %bitcast.25), calls=%async_computation | async-start | bytes 29360128 | tf_op jit(solution)/shard_map/all_to_all | solution.py:33
  32.1 235.4 %all-gather.8.cloned.1.call-start = ((), (), s32[]{:S(2)}) async-start(), calls=%async_computation.5 | async-start | bytes 4128768 | tf_op jit(solution)/shard_map/all_gather | solution.py:49
  32.8 249.9 %all-gather.4.cloned.1.call-start = ((), (), s32[]{:S(2)}) async-start(), calls=%async_computation.2 | async-start | bytes 2621440 | tf_op jit(solution)/shard_map/all_gather | solution.py:32
  39.5 243.3 %all-gather.6.cloned.1.call-start = ((), (), s32[]{:S(2)}) async-start(), calls=%async_computation.4 | async-start | bytes 4718592 | tf_op jit(solution)/shard_map/all_gather | solution.py:48
  40.2 331.2 %reduce-scatter.2.cloned.1.call-start = ((), (), s32[]{:S(2)}) async-start(), calls=%async_computation.3 | async-start | bytes 16515072 | tf_op jit(solution)/shard_map/reduce_scatter | solution.py:34
  266.5 0.7 copy-start
Sparse Core Ops, SparseCore 0:
  34.7 106.9 all-gather.7
  143.3 45.7 all-gather.3
  191.0 41.0 all-gather.5
  266.6 104.8 reduce-scatter.1
where the time goes:
time: 411 us; the launch traced here: 410 us
  waiting for transfers between devices  264 us (64%)
  matrix products  58.8 us (14%)
  local copies, waits for them, and re-layouts  47.9 us (12%)
  between operations  13.8 us (3%)
  blocking collectives  12.2 us (3%)
  other arithmetic  6.67 us (2%)
  starting transfers between devices  5.72 us (1%)
    all_to_all x1, waiting for transfers between devices, per_device(): lax.all_to_all(out_grads, 'dp', split_axis=1, concat_axis=0, tiled=True)  174 us
    reduce_scatter x1, waiting for transfers between devices, per_device(): lax.psum_scatter(jnp.dot(columns, output_basis, preferred_element_type=jn...  88.7 us
    dot_general x1, matrix products, per_device(): jnp.dot(columns, output_basis, preferred_element_type=jnp.float32)  33 us
    unnamed x3, local copies, waits for them, and re-layouts  20 us
    dot_general x1, matrix products, per_device(): jnp.einsum('ri,dij->drj', left_rows, conditioned, preferred_element_type=...  19.2 us
    all_to_all x1, local copies, waits for them, and re-layouts, per_device(): lax.all_to_all(out_grads, 'dp', split_axis=1, concat_axis=0, tiled=True)  18.9 us
    psum x1, blocking collectives, per_device(): return lax.psum(values, 'mp')  12.2 us
    convert_element_type x1, local copies, waits for them, and re-layouts, per_device(): right_part.reshape(number * rank_rows, right_part.shape[2])  8.99 us
  transfers between devices with their start and end apart: 5, of which 2 were waited for; matrix products, arithmetic and copies ran while one was open for 18% of the time, Pallas kernels for 0%

commit v1 on v0

--- a/solution.py
+++ b/solution.py
@@ -30,7 +30,10 @@
         jnp.bfloat16
     )
     rotated_in = lax.all_gather(rotated_share, "mp", axis=1, tiled=True)
-    columns = lax.all_to_all(out_grads, "dp", split_axis=1, concat_axis=0, tiled=True)
+    columns = jnp.concatenate(
+        lax.all_to_all(jnp.stack(jnp.split(out_grads, lax.axis_size("dp"), axis=1)), "dp", 0, 0),
+        axis=0,
+    )
     summed = lax.psum_scatter(
         jnp.dot(columns, output_basis, preferred_element_type=jnp.float32).astype(jnp.bfloat16),
         "dp",

time: 411 us -> 395 us (0.961)
  local copies, waits for them, and re-layouts: 47.9 us -> 32.2 us
    all_to_all x1 -> x0, local copies, waits for them, and re-layouts: 18.9 us -> none  [per_device(): lax.all_to_all(out_grads, 'dp', split_axis=1, concat_axis=0, tiled=True)]
    unnamed x3 -> x9, local copies, waits for them, and re-layouts: 20 us -> 20.2 us
  transfers between devices with their start and end apart: 5 -> 5, of which waited for: 2 -> 2; matrix products, arithmetic and copies ran while one was open for 18% -> 14% of each run, Pallas kernels for 0% -> 0%
where the time goes in v1:
time: 395 us; the launch traced here: 394 us
  waiting for transfers between devices  264 us (67%)
  matrix products  59.5 us (15%)
  local copies, waits for them, and re-layouts  32.2 us (8%)
  between operations  13.8 us (3%)
  blocking collectives  12.2 us (3%)
  other arithmetic  6.67 us (2%)
  starting transfers between devices  5.87 us (1%)
    all_to_all x1, waiting for transfers between devices, per_device(): lax.all_to_all(jnp.stack(jnp.split(out_grads, lax.axis_size('dp'), axis=1...  174 us
    reduce_scatter x1, waiting for transfers between devices, per_device(): lax.psum_scatter(jnp.dot(columns, output_basis, preferred_element_type=jn...  88.6 us
    dot_general x1, matrix products, per_device(): jnp.dot(columns, output_basis, preferred_element_type=jnp.float32)  33.7 us
    unnamed x9, local copies, waits for them, and re-layouts  20.2 us
    dot_general x1, matrix products, per_device(): jnp.einsum('ri,dij->drj', left_rows, conditioned, preferred_element_type=...  19.2 us
    psum x1, blocking collectives, per_device(): return lax.psum(values, 'mp')  12.2 us
    convert_element_type x1, local copies, waits for them, and re-layouts, per_device(): right_part.reshape(number * rank_rows, right_part.shape[2])  9.09 us
  transfers between devices with their start and end apart: 5, of which 2 were waited for; matrix products, arithmetic and copies ran while one was open for 14% of the time, Pallas kernels for 0%

profile of v1, /device:TPU:0, one launch (start us, length us, event | category | flops | bytes accessed | tf_op | source)
XLA Modules:
  0.0 394.4 jit_solution(15562632746858937557)
XLA Ops:
  6.5 2.9 bitcast_dynamic-update-slice_fusion.7
  9.4 2.8 bitcast_dynamic-update-slice_fusion.6
  12.3 2.9 bitcast_dynamic-update-slice_fusion.5
  15.1 2.9 bitcast_dynamic-update-slice_fusion.4
  18.0 2.9 bitcast_dynamic-update-slice_fusion.3
  21.0 2.9 bitcast_dynamic-update-slice_fusion.2
  23.8 2.9 bitcast_dynamic-update-slice_fusion.1
  26.7 2.9 bitcast_dynamic-update-slice_fusion
  29.6 5.5 %all-to-all-start = ((bf16[8,512,1792]{2,1,0:T(8,128)(2,1)}), bf16[8,512,1792]{2,1,0:T(8,128)(2,1)}, u32[]{:S(2)}, u32[]{:S(2)}) async-start(bf16[8,512,1792]{2,1,0:T(8,128)(2,1)} %bitcast_dynamic-update-slice_fusion), calls=%async_computation | async-start | bytes 29360128 | tf_op jit(solution)/shard_map/all_to_all | solution.py:34
  35.2 0.7 all-gather.8.cloned.1.call-update
  35.9 6.6 %convolution_convert_fusion.1 = bf16[512,512]{1,0:T(8,128)(2,1)} fusion(bf16[512,4096]{1,0:T(8,128)(2,1)} %param.11, bf16[4096,512]{1,0:T(8,128)(2,1)} %param.13), kind=kOutput, calls=%fused_computation.17 | convolution fusion | flops 2147745792 | bytes 8912896 | tf_op jit(solution)/shard_map/dot_general | solution.py:29
  42.5 0.0 all-gather.6.cloned.1.call-start
  42.6 0.7 all-gather.6.cloned.1.call-update
  43.3 0.2 reduce-scatter.2.cloned.1.call-start
  43.5 174.1 %all-to-all-done = bf16[8,512,1792]{2,1,0:T(8,128)(2,1)} async-done(((bf16[8,512,1792]{2,1,0:T(8,128)(2,1)}), bf16[8,512,1792]{2,1,0:T(8,128)(2,1)}, u32[]{:S(2)}, u32[]{:S(2)}) %all-to-all-start) | async-done | bytes 14680096 | tf_op jit(solution)/shard_map/all_to_all | solution.py:34
  217.6 33.7 %convolution_convert_fusion = bf16[4096,1792]{1,0:T(8,128)(2,1)} fusion(bf16[4096,1792]{1,0:T(8,128)(2,1)} %bitcast.10, bf16[1792,1792]{1,0:T(8,128)(2,1)} %param.14), kind=kOutput, calls=%fused_computation | convolution fusion | flops 26314014720 | bytes 35782656 | tf_op jit(solution)/shard_map/dot_general | solution.py:38
  252.0 0.3 convert_reduce_fusion
  252.4 6.2 %bitcast_convert_fusion = f32[1,1024,1792]{2,1,0:T(8,128)} fusion(bf16[1,1024,1792]{2,1,0:T(8,128)(2,1)} %bitcast.39), kind=kLoop, calls=%fused_computation.6 | loop fusion | flops 1835008 | bytes 11010048 | tf_op jit(solution)/shard_map/convert_element_type | solution.py:55
  258.6 9.1 %copy.13 = f32[1,1024,1792]{1,2,0:T(8,128)} copy(f32[1,1024,1792]{2,1,0:T(8,128)} %bitcast_convert_fusion) | data formatting | bytes 14680064 | tf_op jit(solution)/shard_map/convert_element_type | solution.py:55
  267.7 88.6 %reduce-scatter.2.cloned.1.call-done = bf16[512,1792]{1,0:T(8,128)(2,1)} async-done(((bf16[4096,1792]{1,0:T(8,128)(2,1)}), bf16[512,1792]{1,0:T(8,128)(2,1)}) %reduce-scatter.2.cloned.1.call-update) | async-done | bytes 1835024 | tf_op jit(solution)/shard_map/reduce_scatter | solution.py:37
  356.3 19.2 %fusion = f32[1024]{0:T(1024)S(1)} fusion(f32[1,1024,1792]{1,2,0:T(8,128)} %copy.13, bf16[1024,2048]{1,0:T(8,128)(2,1)} %bitcast.42, bf16[2048,1792]{1,0:T(8,128)(2,1)} %param.15, bf16[512,2048]{1,0:T(8,128)(2,1)} %all-gather.4.cloned.1.call-done, bf16[512,1792]{1,0:T(8,128)(2,1)} %reduce-scatter.2.cloned.1.call-done, f32[512]{0:T(512)S(1)} %divide_select_fusion), kind=kOutput, calls=%fused_computation.3 | convolution fusion | flops 11295390720 | bytes 22812672 | tf_op jit(solution)/shard_map/ri,dij->drj/dot_general | solution.py:56
  375.5 0.1 reduce_sum.29
  375.6 0.1 reduce_sum.30
  375.7 12.2 %psum.7 = f32[1,32]{1,0:T(1,128)} all-reduce(f32[1,32]{1,0:T(1,128)S(1)} %bitcast.41), channel_id=1, replica_groups=mesh['dp'=8,'mp'=4] {'mp'}, use_global_device_ids=true, to_apply=%region_4.5 | all-reduce | flops 32 | bytes 256 | tf_op jit(solution)/shard_map/psum | solution.py:58
  (11 shorter events, 0.2 us)
Async XLA Ops:
  29.6 188.1 %all-to-all-start = ((bf16[8,512,1792]{2,1,0:T(8,128)(2,1)}), bf16[8,512,1792]{2,1,0:T(8,128)(2,1)}, u32[]{:S(2)}, u32[]{:S(2)}) async-start(bf16[8,512,1792]{2,1,0:T(8,128)(2,1)} %bitcast_dynamic-update-slice_fusion), calls=%async_computation | async-start | bytes 29360128 | tf_op jit(solution)/shard_map/all_to_all | solution.py:34
  35.1 217.3 %all-gather.8.cloned.1.call-start = ((), (), s32[]{:S(2)}) async-start(), calls=%async_computation.5 | async-start | bytes 4128768 | tf_op jit(solution)/shard_map/all_gather | solution.py:52
  35.9 231.9 %all-gather.4.cloned.1.call-start = ((), (), s32[]{:S(2)}) async-start(), calls=%async_computation.2 | async-start | bytes 2621440 | tf_op jit(solution)/shard_map/all_gather | solution.py:32
  42.5 225.2 %all-gather.6.cloned.1.call-start = ((), (), s32[]{:S(2)}) async-start(), calls=%async_computation.4 | async-start | bytes 4718592 | tf_op jit(solution)/shard_map/all_gather | solution.py:51
  43.3 313.0 %reduce-scatter.2.cloned.1.call-start = ((), (), s32[]{:S(2)}) async-start(), calls=%async_computation.3 | async-start | bytes 16515072 | tf_op jit(solution)/shard_map/reduce_scatter | solution.py:37
  251.3 0.7 copy-start
Sparse Core Ops, SparseCore 0:
  37.8 106.9 all-gather.7
  146.4 45.7 all-gather.3
  194.1 41.0 all-gather.5
  251.5 104.7 reduce-scatter.1
